TPU v7x, 32 devices: a whole 2x2x4 slice. The times are simulated.
32 devices in a mesh: rep: 2 (over x), slab: 8 (over z, y), pix: 2 (over core).
Axes of the slice: x: 2, y: 2, z: 4, core: 2. Of those that a mesh axis runs over, the one named last changes fastest.
Arguments:
- projections: bfloat16 [16, 256, 512], P(('rep', 'pix'), 'slab'), may hold values from -6 to 6
- ctf_weight: bfloat16 [16, 256, 256], P(('rep', 'pix'), 'slab'), may hold values from 0.099609375 to 4
- orient: int32 [16], P(('rep', 'pix')), may hold values from 0 to 63
- angle_table: int32 [64, 4, 256], replicated, may hold values from 0 to 255, as said below
Outputs:
- density: float32 [256, 256, 512], P(('rep', 'pix'), 'slab')
Inputs may be any that keep to these rules, and one draw needn't show every extreme that they name: `angle_table`: for every entry and column, the lower indices lie between 3 and 253, and the fractions between 0 and 255.
All inputs are finite; a program needn't handle non-finite values.
Results may differ from a plain program's by a relative error of at most 0.0022.
Values may be sent and summed in bfloat16 or wider, within the bound.
No kernel may reach another device: no remote copies, remote signals or barrier semaphores. Data moves between devices by JAX's collectives and lax.ppermute only.
A program may use at most 128 MiB of HBM per device.

v0:
```python
import jax
import jax.numpy as jnp
from jax import lax
from jax.sharding import PartitionSpec as P


def corner_weights(first_index, index_count, lower_index, fraction):
    indices = first_index + lax.iota(jnp.int32, index_count)
    lower_hit = (indices[:, None, None] == lower_index[None, :, :]).astype(jnp.float32)
    upper_hit = (indices[:, None, None] == lower_index[None, :, :] + 1).astype(jnp.float32)
    fraction_weight = fraction.astype(jnp.float32)[None, :, :] / 256.0
    return lower_hit * (1.0 - fraction_weight) + upper_hit * fraction_weight


def lookup(orient, angle_table):
    choose = (orient[:, None] == lax.iota(jnp.int32, angle_table.shape[0])[None, :]).astype(
        jnp.int32
    )
    return jnp.sum(choose[:, :, None, None] * angle_table[None], axis=1)


def spread(samples, geometry, first_x, count_x, first_z, count_z, block_rows):
    flat_samples = samples.reshape(samples.shape[0] * samples.shape[1], samples.shape[2])
    weights_third = corner_weights(first_z, count_z, geometry[:, 2], geometry[:, 3])
    block_count = count_x // block_rows

    def one_block(block_start):
        weights_first = corner_weights(block_start, block_rows, geometry[:, 0], geometry[:, 1])
        matrix = (weights_first[:, None, :, :] * weights_third[None, :, :, :]).astype(jnp.bfloat16)
        matrix = matrix.reshape(block_rows * count_z, flat_samples.shape[0])
        summed = jnp.dot(matrix, flat_samples, preferred_element_type=jnp.float32)
        return summed.reshape(block_rows, count_z, samples.shape[2])

    starts = first_x + block_rows * lax.iota(jnp.int32, block_count)
    blocks = lax.map(one_block, starts)
    return blocks.reshape(count_x, count_z, samples.shape[2])


def body(projections, ctf_weight, orient, angle_table):
    planes = projections.shape[1]
    columns = projections.shape[2] // 2
    owned_rows = columns // (lax.axis_size("rep") * lax.axis_size("pix"))
    first_plane = lax.axis_index("slab") * planes
    first_row = (lax.axis_index("rep") * lax.axis_size("pix") + lax.axis_index("pix")) * owned_rows
    whole_proj, whole_ctf = (
        lax.all_gather(projections, "slab", axis=1, tiled=True),
        lax.all_gather(ctf_weight, "slab", axis=1, tiled=True),
    )
    samples = jnp.concatenate([whole_proj, whole_ctf], axis=2)
    geometry = lookup(lax.all_gather(orient, ("rep", "pix"), axis=0, tiled=True), angle_table)
    volume_block = spread(
        lax.all_gather(samples, ("rep", "pix"), axis=0, tiled=True),
        geometry,
        first_row,
        owned_rows,
        first_plane,
        planes,
        owned_rows,
    )
    values = volume_block[:, :, : 2 * columns].reshape(owned_rows, planes, 2, columns)
    density = volume_block[:, :, None, 2 * columns :] + 1.0
    return (values / density).reshape(owned_rows, planes, 2 * columns)


def solution(mesh):
    placed = (
        P(("rep", "pix"), "slab", None),
        P(("rep", "pix"), "slab", None),
        P(("rep", "pix")),
        P(),
    )
    return jax.shard_map(
        body, mesh=mesh, in_specs=placed, out_specs=P(("rep", "pix"), "slab", None), check_vma=False
    )
```

profile of v0, /device:TPU:18, one launch (start us, length us, event | category | flops | bytes accessed | tf_op | source)
XLA Modules:
  0.0 147.8 jit_solution(16701713103617546590)
XLA Ops:
  6.5 0.0 copy-start.3
  6.5 0.0 copy-start.1
  6.5 0.0 copy-start.2
  6.5 0.0 all-gather.3.cloned.1.call-start
  6.5 0.7 all-gather.3.cloned.1.call-update
  7.3 0.0 all-gather.5.cloned.1.call-start
  7.3 27.5 %all_gather.14 = bf16[4,256,256]{2,1,0:T(8,128)(2,1)S(1)} all-gather(bf16[4,32,256]{2,1,0:T(8,128)(2,1)} %param.5), channel_id=1, replica_groups=mesh['rep'=2,'slab'=8,'pix'=2] {'slab'}, dimensions={1}, use_global_device_ids=true | all-gather | bytes 589824 | tf_op jit(solution)/shard_map/all_gather | solution.py:47
  34.8 15.3 %all-gather.3.cloned.1.call-done = bf16[4,256,512]{2,1,0:T(8,128)(2,1)} async-done(((bf16[4,32,512]{2,1,0:T(8,128)(2,1)}), bf16[4,256,512]{2,1,0:T(8,128)(2,1)}) %all-gather.3.cloned.1.call-update) | async-done | bytes 1048592 | tf_op jit(solution)/shard_map/all_gather | solution.py:46
  50.1 2.5 %pad_maximum_fusion = bf16[4,256,768]{2,1,0:T(8,128)(2,1)} fusion(bf16[4,256,256]{2,1,0:T(8,128)(2,1)S(1)} %all_gather.14, bf16[4,256,512]{2,1,0:T(8,128)(2,1)} %all-gather.3.cloned.1.call-done), kind=kLoop, calls=%fused_computation.9 | loop fusion | flops 3145728 | bytes 3145728 | tf_op jit(solution)/shard_map/concatenate | solution.py:49
  52.6 0.0 all-gather.5.cloned.1.call-update
  52.6 0.0 copy-done.1
  52.6 0.1 copy.5
  52.7 0.0 copy-done.3
  52.7 0.6 dynamic-slice
  53.8 0.0 copy-done.2
  53.8 0.2 dynamic-update-slice
  54.1 4.3 %all-reduce = s32[16]{0:T(128)S(1)} all-reduce(s32[16]{0:T(128)S(1)} %dynamic-update-slice), channel_id=1, replica_groups=mesh['rep'=2,'slab'=8,'pix'=2] {'rep','pix'}, use_global_device_ids=true, to_apply=%add | all-reduce | flops 16 | bytes 128
  58.3 0.1 fusion.10
  58.4 0.8 multiply_reduce_fusion
  59.4 0.2 select_add_fusion.1
  59.5 0.2 select_add_fusion
  59.8 39.2 %all-gather.5.cloned.1.call-done = bf16[16,256,768]{2,1,0:T(8,128)(2,1)} async-done(((bf16[4,256,768]{2,1,0:T(8,128)(2,1)}), bf16[16,256,768]{2,1,0:T(8,128)(2,1)}) %all-gather.5.cloned.1.call-update) | async-done | bytes 6291472 | tf_op jit(solution)/shard_map/all_gather | solution.py:52
  99.0 22.4 %fusion.4 = f32[64,32,768]{2,1,0:T(8,128)S(1)} fusion(bf16[16,256,768]{2,1,0:T(8,128)(2,1)} %all-gather.5.cloned.1.call-done, f32[32,16,256]{2,0,1:T(8,128)S(1)} %select_add_fusion.1, f32[64,16,256]{2,1,0:T(8,128)S(1)} %select_add_fusion), kind=kOutput, calls=%fused_computation.7 | convolution fusion | flops 12901679104 | bytes 14155776 | tf_op jit(solution)/shard_map/while/body/eval_jaxpr/dot_general | solution.py:31
  121.3 0.0 copy-start
  121.3 2.6 %copy-done = f32[64,32,768]{2,1,0:T(8,128)} copy-done((f32[64,32,768]{2,1,0:T(8,128)}, f32[64,32,768]{2,1,0:T(8,128)S(1)}, u32[]{:S(2)}) %copy-start) | copy-done | bytes 6291480
  124.0 0.2 slice_add_fusion
  124.2 3.5 %div.26 = f32[64,32,2,256]{3,2,1,0:T(2,128)} broadcast(f32[64,32,256]{2,1,0:T(8,128)S(1)} %slice_add_fusion), dimensions={0,1,3} | broadcast | bytes 6291456 | tf_op jit(solution)/shard_map/div | solution.py:62
  127.7 6.4 %div.27 = f32[64,32,512]{2,1,0:T(8,128)} reshape(f32[64,32,2,256]{3,2,1,0:T(2,128)} %div.26) | data formatting | bytes 8388608 | tf_op jit(solution)/shard_map/div | solution.py:62
  134.1 6.9 %slice_divide_fusion = f32[64,32,512]{2,1,0:T(8,128)} fusion(f32[64,32,512]{2,1,0:T(8,128)} %div.27, f32[64,32,768]{2,1,0:T(8,128)} %copy-done), kind=kLoop, calls=%fused_computation.5 | loop fusion | flops 1048576 | bytes 12582912 | tf_op jit(solution)/shard_map/div | solution.py:62
  (11 shorter events, 0.1 us)
Async XLA Ops:
  6.5 46.2 %copy-start.3 = (u32[32]{0:T(128)S(1)}, u32[32]{0:T(128)}, u32[]{:S(2)}) copy-start(u32[32]{0:T(128)} %constant.48) | copy-start | bytes 388
  6.5 46.1 %copy-start.1 = (s32[64,4,256]{2,1,0:T(4,128)S(1)}, s32[64,4,256]{2,1,0:T(4,128)}, u32[]{:S(2)}) copy-start(s32[64,4,256]{2,1,0:T(4,128)} %param.7) | copy-start | bytes 786436
  6.5 47.3 %copy-start.2 = (s32[4]{0:T(128)S(1)}, s32[4]{0:T(128)}, u32[]{:S(2)}) copy-start(s32[4]{0:T(128)} %param.6) | copy-start | bytes 52
  6.5 43.6 %all-gather.3.cloned.1.call-start = ((), (), s32[]{:S(2)}) async-start(), calls=%async_computation | async-start | bytes 1179648 | tf_op jit(solution)/shard_map/all_gather | solution.py:46
  7.3 91.7 %all-gather.5.cloned.1.call-start = ((), (), s32[]{:S(2)}) async-start(), calls=%async_computation.1 | async-start | bytes 7864320 | tf_op jit(solution)/shard_map/all_gather | solution.py:52
  121.3 2.7 %copy-start = (f32[64,32,768]{2,1,0:T(8,128)}, f32[64,32,768]{2,1,0:T(8,128)S(1)}, u32[]{:S(2)}) copy-start(f32[64,32,768]{2,1,0:T(8,128)S(1)} %fusion.4) | copy-start | bytes 18874372
Sparse Core Ops, SparseCore 0:
  9.5 40.5 all-gather.2
  52.7 46.1 all-gather.4
where the time goes:
time: 151 us; the launch traced here: 148 us
  waiting for transfers between devices  55.2 us (37%)
  blocking collectives  31.8 us (21%)
  matrix products  22.4 us (15%)
  between operations  14.1 us (9%)
  local copies, waits for them, and re-layouts  13.5 us (9%)
  other arithmetic  10.8 us (7%)
    all_gather x1, waiting for transfers between devices, body(): lax.all_gather(samples, ('rep', 'pix'), axis=0, tiled=True)  39.2 us
    all_gather x1, blocking collectives, body(): lax.all_gather(ctf_weight, 'slab', axis=1, tiled=True)  27.5 us
    dot_general x1, matrix products, one_block(): summed = jnp.dot(matrix, flat_samples, preferred_element_type=jnp.float32)  22.4 us
    all_gather x1, waiting for transfers between devices, body(): lax.all_gather(projections, 'slab', axis=1, tiled=True)  15.3 us
    div x2, local copies, waits for them, and re-layouts, body(): return (values / density).reshape(owned_rows, planes, 2 * columns)  9.9 us
    div x1, other arithmetic, body(): return (values / density).reshape(owned_rows, planes, 2 * columns)  6.89 us
    unnamed x1, blocking collectives  4.27 us
    unnamed x13, local copies, waits for them, and re-layouts  3.52 us
  transfers between devices with their start and end apart: 2, of which 2 were waited for; matrix products, arithmetic and copies ran while one was open for 1% of the time, Pallas kernels for 0%

commit v1 on v0

v1 whole, which is shorter than its diff:
```python
import jax
import jax.numpy as jnp
import numpy as np
from jax import lax
from jax.experimental import pallas as pl
from jax.experimental.pallas import tpu as pltpu
from jax.sharding import PartitionSpec as P

BATCH_AXES = ("rep", "pix")
GROUP = 16
TILE = 256
LANES = 128

SCHEDULE = (
    ("x", "100", "000"), ("y", "010", "000"), ("z", "001", "000"),
    ("x", "101", "001"), ("y", "110", "100"), ("z", "002", "001"),
    ("x", "102", "002"), ("y", "012", "002"), ("z", "003", "002"),
    ("x", "103", "003"), ("y", "013", "003"), ("z", "111", "110"),
    ("x", "113", "013"), ("y", "011", "001"), ("z", "112", "111"),
)


class Ports:
    def __init__(self, mesh):
        self.rep, self.slab, self.pix = (mesh.shape[a] for a in ("rep", "slab", "pix"))

    def fits(self):
        return (self.rep, self.slab, self.pix) == (2, 8, 2)

    def pairs(self, port):
        if port == "x":
            return "rep", [(i, 1 - i) for i in range(self.rep)]
        if port == "y":
            return "slab", [(i, i ^ 1) for i in range(self.slab)]
        if port == "z":
            return "slab", [(i, (i + 2) % self.slab) for i in range(self.slab)]
        return "pix", [(i, 1 - i) for i in range(self.pix)]

    def send(self, value, port):
        axis, pairs = self.pairs(port)
        return lax.ppermute(value, axis, pairs)

    def move(self, owner, port):
        axis, pairs = self.pairs(port)
        dim = ("rep", "slab", "pix").index(axis)
        moved = np.empty_like(owner)
        for source, target in pairs:
            to, frm = [slice(None)] * 3, [slice(None)] * 3
            to[dim], frm[dim] = target, source
            moved[tuple(to)] = owner[tuple(frm)]
        return moved


def gather_pieces(samples, ports):
    first = np.arange(ports.rep * ports.slab * ports.pix).reshape(ports.rep, ports.slab, ports.pix)
    held = {"000": (samples, first)}
    for port, name, source in SCHEDULE:
        value, owner = held[source]
        held[name] = (ports.send(value, port), ports.move(owner, port))
    pieces = list(held.values())
    pieces += [(ports.send(v, "core"), ports.move(o, "core")) for v, o in pieces]
    owners = np.stack([o for _, o in pieces], axis=-1)
    assert (np.sort(owners, -1) == np.arange(first.size)).all()
    return [v for v, _ in pieces], owners


def lookup(orient, angle_table):
    choose = (orient[:, None] == lax.iota(jnp.int32, angle_table.shape[0])[None, :]).astype(jnp.int32)
    return jnp.sum(choose[:, :, None, None] * angle_table[None], axis=1)


def corner(indices, lower, fraction):
    return jnp.where(indices == lower, 1.0 - fraction, 0.0) + jnp.where(indices == lower + 1, fraction, 0.0)


def spread(pieces, place, active, geometry, box, count_x, count_z, columns, per_piece):
    batch, width = per_piece
    pieces_n = len(pieces)
    groups = width // GROUP
    segments = pieces_n * batch * groups
    rows_max = segments * GROUP
    row_block = TILE // count_z
    steps = count_x // row_block
    channels = 3 * columns
    lane_groups = LANES // GROUP

    def kernel(*refs):
        box_ref, place_ref, active_ref, geometry_ref = refs[:4]
        piece_refs = refs[4 : 4 + pieces_n]
        out_ref = refs[4 + pieces_n]
        compact, listed, where, total, staged, sems = refs[5 + pieces_n :]
        first_x, first_z = box_ref[0], box_ref[1]

        count = jnp.int32(0)
        for index, piece in enumerate(piece_refs):
            first_n, first_group = place_ref[2 * index], place_ref[2 * index + 1]

            def take(item, count, piece=piece, first_n=first_n, first_group=first_group):
                name = (first_n + item // groups) * (columns // GROUP) + first_group + item % groups
                hit = active_ref[name]

                @pl.when(hit > 0)
                def _():
                    source = pl.ds(pl.multiple_of(item * GROUP, GROUP), GROUP)
                    target = pl.ds(pl.multiple_of(count * GROUP, GROUP), GROUP)
                    compact[target, :] = piece[source, :]
                    listed[count] = name

                return count + hit

            count = lax.fori_loop(0, batch * groups, take, count)

        tiles = (count * GROUP + TILE - 1) // TILE

        def clear(item, carry):
            target = pl.ds(pl.multiple_of(item * GROUP, GROUP), GROUP)
            compact[target, :] = jnp.zeros((GROUP, channels), jnp.bfloat16)
            return carry

        lax.fori_loop(count, tiles * (TILE // GROUP), clear, 0)

        lane_group = lax.broadcasted_iota(jnp.int32, (8, LANES), 1) // GROUP

        def order(block, carry):
            gathered = jnp.full((8, LANES), -4.0, jnp.float32)
            for slot in range(lane_groups):
                item = block * lane_groups + slot
                valid = item < count
                name = listed[jnp.minimum(item, count - 1)]
                n, group = name // (columns // GROUP), name % (columns // GROUP)
                lanes = pl.ds(pl.multiple_of(group // lane_groups * LANES, LANES), LANES)
                source = geometry_ref[n, :, lanes]
                shift = lax.rem(slot - lax.rem(group, lane_groups) + lane_groups, lane_groups) * GROUP
                rolled = pltpu.roll(source, shift, 1)
                gathered = jnp.where((lane_group == slot) & valid, rolled, gathered)
            where[:, pl.ds(pl.multiple_of(block * LANES, LANES), LANES)] = gathered
            return carry

        lax.fori_loop(0, tiles * (TILE // LANES), order, 0)

        def out_copy(step, slot):
            rows = pl.ds(step * row_block, row_block)
            return pltpu.make_async_copy(staged.at[slot], out_ref.at[rows], sems.at[slot])

        for step in range(steps):
            slot = step % 2
            total[...] = jnp.zeros_like(total)

            def add(tile, carry, step=step):
                lanes = pl.ds(pl.multiple_of(tile * TILE, TILE), TILE)
                lower_x, part_x = where[0:1, lanes], where[1:2, lanes]
                lower_z, part_z = where[2:3, lanes], where[3:4, lanes]
                at_x = (first_x + step * row_block + lax.broadcasted_iota(jnp.int32, (row_block, TILE), 0)).astype(jnp.float32)
                at_z = (first_z + lax.broadcasted_iota(jnp.int32, (count_z, TILE), 0)).astype(jnp.float32)
                weight_x = corner(at_x, lower_x, part_x)
                weight_z = corner(at_z, lower_z, part_z)
                matrix = (weight_x[:, None, :] * weight_z[None, :, :]).astype(jnp.bfloat16)
                matrix = matrix.reshape(row_block * count_z, TILE)
                total[...] += jnp.dot(matrix, compact[lanes, :], preferred_element_type=jnp.float32)
                return carry

            lax.fori_loop(0, tiles, add, 0)
            if step >= 2:
                out_copy(step - 2, slot).wait()
            scale = 1.0 / (total[:, 2 * columns :] + 1.0)
            shape = (row_block, count_z, columns)
            staged[slot, :, :, :columns] = (total[:, :columns] * scale).reshape(shape)
            staged[slot, :, :, columns:] = (total[:, columns : 2 * columns] * scale).reshape(shape)
            out_copy(step, slot).start()
        for step in range(max(steps - 2, 0), steps):
            out_copy(step, step % 2).wait()

    smem, vmem = pl.BlockSpec(memory_space=pltpu.SMEM), pl.BlockSpec(memory_space=pltpu.VMEM)
    return pl.pallas_call(
        kernel,
        out_shape=jax.ShapeDtypeStruct((count_x, count_z, 2 * columns), jnp.float32),
        in_specs=[smem, smem, smem, vmem] + [vmem] * pieces_n,
        out_specs=pl.BlockSpec(memory_space=pl.ANY),
        scratch_shapes=[
            pltpu.VMEM((rows_max, channels), jnp.bfloat16),
            pltpu.SMEM((segments,), jnp.int32),
            pltpu.VMEM((8, rows_max), jnp.float32),
            pltpu.VMEM((row_block * count_z, channels), jnp.float32),
            pltpu.VMEM((2, row_block, count_z, 2 * columns), jnp.float32),
            pltpu.SemaphoreType.DMA((2,)),
        ],
        compiler_params=pltpu.CompilerParams(vmem_limit_bytes=20 << 20),
        name="spread",
    )(box, place, active, geometry, *pieces)


def make_body(ports):
    def body(projections, ctf_weight, orient, angle_table):
        batch, planes = projections.shape[:2]
        columns = projections.shape[2] // 2
        owned_rows = columns // (ports.rep * ports.pix)
        first_z = lax.axis_index("slab") * planes
        first_x = (lax.axis_index("rep") * ports.pix + lax.axis_index("pix")) * owned_rows
        samples = jnp.concatenate([projections, ctf_weight], axis=2).reshape(batch * planes, 3 * columns)
        pieces, owners = gather_pieces(samples, ports)

        geometry = lookup(lax.all_gather(orient, BATCH_AXES, axis=0, tiled=True), angle_table)
        lower_x, lower_z = geometry[:, 0], geometry[:, 2]
        hit = (lower_x >= first_x - 1) & (lower_x < first_x + owned_rows)
        hit &= (lower_z >= first_z - 1) & (lower_z < first_z + planes)
        active = jnp.any(hit.reshape(-1, GROUP), axis=1).astype(jnp.int32)
        unit = jnp.array([1.0, 1.0 / 256.0, 1.0, 1.0 / 256.0], jnp.float32)
        table = jnp.pad(geometry.astype(jnp.float32) * unit[None, :, None], ((0, 0), (0, 4), (0, 0)))

        owner_rep, owner_slab, owner_pix = np.unravel_index(owners, owners.shape[:3])
        place = np.stack([(owner_rep * ports.pix + owner_pix) * batch, owner_slab * (planes // GROUP)], -1)
        place = jnp.asarray(place.reshape(-1, place.shape[-2] * 2), jnp.int32)
        me = (lax.axis_index("rep") * ports.slab + lax.axis_index("slab")) * ports.pix + lax.axis_index("pix")
        place = lax.dynamic_index_in_dim(place, me, 0, keepdims=False)
        box = jnp.stack([first_x, first_z]).astype(jnp.int32)
        return spread(pieces, place, active, table, box, owned_rows, planes, columns, (batch, planes))

    return body


def plain_body(projections, ctf_weight, orient, angle_table):
    planes = projections.shape[1]
    columns = projections.shape[2] // 2
    owned_rows = columns // (lax.axis_size("rep") * lax.axis_size("pix"))
    first_z = lax.axis_index("slab") * planes
    first_x = (lax.axis_index("rep") * lax.axis_size("pix") + lax.axis_index("pix")) * owned_rows
    samples = jnp.concatenate([projections, ctf_weight], axis=2)
    samples = lax.all_gather(samples, "slab", axis=1, tiled=True)
    samples = lax.all_gather(samples, BATCH_AXES, axis=0, tiled=True)
    geometry = lookup(lax.all_gather(orient, BATCH_AXES, axis=0, tiled=True), angle_table)
    geometry = geometry.astype(jnp.float32)
    at_x = (first_x + lax.iota(jnp.int32, owned_rows)).astype(jnp.float32)[:, None, None]
    at_z = (first_z + lax.iota(jnp.int32, planes)).astype(jnp.float32)[:, None, None]
    weight_x = corner(at_x, geometry[None, :, 0], geometry[None, :, 1] / 256.0)
    weight_z = corner(at_z, geometry[None, :, 2], geometry[None, :, 3] / 256.0)
    matrix = (weight_x[:, None] * weight_z[None]).astype(jnp.bfloat16).reshape(owned_rows * planes, -1)
    volume = jnp.dot(matrix, samples.reshape(-1, 3 * columns), preferred_element_type=jnp.float32)
    values = volume[:, : 2 * columns].reshape(-1, 2, columns) / (volume[:, None, 2 * columns :] + 1.0)
    return values.reshape(owned_rows, planes, 2 * columns)


def solution(mesh):
    placed = (
        P(BATCH_AXES, "slab", None),
        P(BATCH_AXES, "slab", None),
        P(BATCH_AXES),
        P(),
    )
    ports = Ports(mesh)
    body = make_body(ports) if ports.fits() else plain_body
    return jax.shard_map(
        body, mesh=mesh, in_specs=placed, out_specs=P(BATCH_AXES, "slab", None), check_vma=False
    )
```

time: 151 us -> 67.2 us (0.45); the launches traced: 148 us -> 66.8 us
  waiting for transfers between devices: 55.2 us -> 12 us
  blocking collectives: 31.8 us -> 4.27 us
  starting transfers between devices: 0.04 us -> 23 us
  matrix products: 22.4 us -> 0 us
  Pallas kernels: 0 us -> 18.5 us
  between operations: 14.1 us -> 0.8 us
  local copies, waits for them, and re-layouts: 13.5 us -> 4.56 us
  other arithmetic: 10.8 us -> 3.65 us
    all_gather x2 -> x0, waiting for transfers between devices: 54.5 us -> none  [the longest x1 39.2 us: body(): lax.all_gather(samples, ('rep', 'pix'), axis=0, tiled=True)]
    all_gather x1 -> x0, blocking collectives: 27.5 us -> none  [body(): lax.all_gather(ctf_weight, 'slab', axis=1, tiled=True)]
    ppermute x0 -> x31, starting transfers between devices: none -> 23 us  [send(): return lax.ppermute(value, axis, pairs)]
    dot_general x1 -> x0, matrix products: 22.4 us -> none  [one_block(): summed = jnp.dot(matrix, flat_samples, preferred_element_type=jnp.float32)]
    pallas_call x0 -> x1, Pallas kernels: none -> 18.5 us  [spread(): pl.pallas_call(kernel, out_shape=jax.ShapeDtypeStruct((count_x, count_z,...]
    ppermute x0 -> x31, waiting for transfers between devices: none -> 12 us  [send(): return lax.ppermute(value, axis, pairs)]
    div x2 -> x0, local copies, waits for them, and re-layouts: 9.9 us -> none  [body(): return (values / density).reshape(owned_rows, planes, 2 * columns)]
    div x3 -> x0, other arithmetic: 6.92 us -> none  [the longest x1 6.89 us: body(): return (values / density).reshape(owned_rows, planes, 2 * columns)]
  transfers between devices with their start and end apart: 2 -> 31, of which waited for: 2 -> 8; matrix products, arithmetic and copies ran while one was open for 1% -> 11% of each run, Pallas kernels for 0% -> 0%
where the time goes in v1:
time: 67.2 us; the launch traced here: 66.8 us
  starting transfers between devices  23 us (34%)
  Pallas kernels  18.5 us (28%)
  waiting for transfers between devices  12 us (18%)
  local copies, waits for them, and re-layouts  4.56 us (7%)
  blocking collectives  4.27 us (6%)
  other arithmetic  3.65 us (5%)
  between operations  0.8 us (1%)
    ppermute x31, starting transfers between devices, send(): return lax.ppermute(value, axis, pairs)  23 us
    pallas_call x1, Pallas kernels, spread(): pl.pallas_call(kernel, out_shape=jax.ShapeDtypeStruct((count_x, count_z,...  18.5 us
    ppermute x31, waiting for transfers between devices, send(): return lax.ppermute(value, axis, pairs)  12 us
    unnamed x1, blocking collectives  4.27 us
    unnamed x6, local copies, waits for them, and re-layouts  3.1 us
  transfers between devices with their start and end apart: 31, of which 8 were waited for; matrix products, arithmetic and copies ran while one was open for 11% of the time, Pallas kernels for 0%

profile of v1, /device:TPU:18, one launch (start us, length us, event | category | flops | bytes accessed | tf_op | source)
XLA Modules:
  0.0 66.8 jit_solution(6878865708800988066)
XLA Ops:
  0.0 1.0 %pad_maximum_fusion = bf16[4,32,768]{2,1,0:T(8,128)(2,1)S(1)} fusion(bf16[4,32,256]{2,1,0:T(8,128)(2,1)} %param.7, bf16[4,32,512]{2,1,0:T(8,128)(2,1)} %param.6), kind=kLoop, calls=%fused_computation.1 | loop fusion | flops 393216 | bytes 393216 | tf_op jit(solution)/shard_map/concatenate | solution.py:199
  1.0 1.6 %collective-permute-start.2 = (bf16[128,768]{1,0:T(8,128)(2,1)S(1)}, bf16[128,768]{1,0:T(8,128)(2,1)S(1)}, u32[]{:S(2)}, u32[]{:S(2)}) collective-permute-start(bf16[128,768]{1,0:T(8,128)(2,1)S(1)} %bitcast.8), channel_id=1, source_target_pairs={{0,4},{2,6},{4,8},{6,10},{8,12},{10,14},{12,0},{14,2},{1,5},{3,7},... | collective-permute-start | bytes 589832 | tf_op jit(solution)/shard_map/ppermute | solution.py:41
  2.6 1.5 %collective-permute-start.1 = (bf16[128,768]{1,0:T(8,128)(2,1)S(1)}, bf16[128,768]{1,0:T(8,128)(2,1)S(1)}, u32[]{:S(2)}, u32[]{:S(2)}) collective-permute-start(bf16[128,768]{1,0:T(8,128)(2,1)S(1)} %bitcast.10), channel_id=1, source_target_pairs={{0,2},{2,0},{4,6},{6,4},{8,10},{10,8},{12,14},{14,12},{1,3},{3,1},... | collective-permute-start | bytes 589832 | tf_op jit(solution)/shard_map/ppermute | solution.py:41
  4.6 3.0 %collective-permute-done.2.refs_7_ = bf16[128,768]{1,0:T(8,128)(2,1)S(1)} collective-permute-done((bf16[128,768]{1,0:T(8,128)(2,1)S(1)}, bf16[128,768]{1,0:T(8,128)(2,1)S(1)}, u32[]{:S(2)}, u32[]{:S(2)}) %collective-permute-start.2) | collective-permute-done | bytes 196640 | tf_op jit(solution)/shard_map/ppermute | solution.py:41
  7.7 1.5 %collective-permute-start.13 = (bf16[128,768]{1,0:T(8,128)(2,1)S(1)}, bf16[128,768]{1,0:T(8,128)(2,1)S(1)}, u32[]{:S(2)}, u32[]{:S(2)}) collective-permute-start(bf16[128,768]{1,0:T(8,128)(2,1)S(1)} %collective-permute-done.2.refs_7_), channel_id=1, source_target_pairs={{0,2},{2,0},{4,6},{6,4},{8,10},{10,8},{12,14},{14,12},{1,3},{3,1},... | collective-permute-start | bytes 589832 | tf_op jit(solution)/shard_map/ppermute | solution.py:41
  9.2 1.2 %dynamic-slice = u32[1]{0:T(128)} dynamic-slice(u32[32]{0:T(128)} %constant.44, u32[]{:T(128)S(6)} %add.29), dynamic_slice_sizes={1} | dynamic-slice | bytes 12
  11.1 0.9 %dynamic-update-slice = s32[16]{0:T(128)S(1)} dynamic-update-slice(s32[16]{0:T(128)S(1)} %broadcast.30, s32[4]{0:T(128)} %param.8, u32[]{:T(128)} %bitcast.3) | dynamic-update-slice | bytes 36
  11.9 4.3 %all-reduce.1 = s32[16]{0:T(128)S(1)} all-reduce(s32[16]{0:T(128)S(1)} %dynamic-update-slice), channel_id=1, replica_groups=mesh['rep'=2,'slab'=8,'pix'=2] {'rep','pix'}, use_global_device_ids=true, to_apply=%add.1 | all-reduce | flops 16 | bytes 128
  16.2 1.6 %collective-permute-start.5 = (bf16[128,768]{1,0:T(8,128)(2,1)S(1)}, bf16[128,768]{1,0:T(8,128)(2,1)S(1)}, u32[]{:S(2)}, u32[]{:S(2)}) collective-permute-start(bf16[128,768]{1,0:T(8,128)(2,1)S(1)} %collective-permute-done.2.refs_7_), channel_id=1, source_target_pairs={{0,4},{2,6},{4,8},{6,10},{8,12},{10,14},{12,0},{14,2},{1,5},{3,7},... | collective-permute-start | bytes 589832 | tf_op jit(solution)/shard_map/ppermute | solution.py:41
  17.8 1.1 %collective-permute-start.3 = (bf16[128,768]{1,0:T(8,128)(2,1)S(1)}, bf16[128,768]{1,0:T(8,128)(2,1)S(1)}, u32[]{:S(2)}, u32[]{:S(2)}) collective-permute-start(bf16[128,768]{1,0:T(8,128)(2,1)S(1)} %collective-permute-done.2.refs_7_), channel_id=1, source_target_pairs={{0,16},{16,0},{1,17},{17,1},{2,18},{18,2},{3,19},{19,3},{4,20},{20... | collective-permute-start | bytes 589832 | tf_op jit(solution)/shard_map/ppermute | solution.py:41
  19.0 0.6 collective-permute-start.4
  19.8 1.0 %copy.8 = s32[64,4,256]{2,0,1:T(8,128)S(1)} copy(s32[64,4,256]{2,1,0:T(4,128)} %param.9) | data formatting | bytes 524288 | tf_op args[3]
  20.8 0.8 %multiply_reduce_fusion = s32[16,4,256]{2,1,0:T(4,128)S(1)} fusion(s32[64,4,256]{2,0,1:T(8,128)S(1)} %copy.8, s32[16,64]{1,0:T(8,128)S(1)} %fusion), kind=kLoop, calls=%fused_computation | loop fusion | flops 2080768 | bytes 331776 | tf_op jit(solution)/shard_map/reduce_sum | solution.py:69
  21.6 0.6 collective-permute-done.5.refs_10_
  22.1 1.4 %collective-permute-done.3.refs_8_ = bf16[128,768]{1,0:T(8,128)(2,1)S(1)} collective-permute-done((bf16[128,768]{1,0:T(8,128)(2,1)S(1)}, bf16[128,768]{1,0:T(8,128)(2,1)S(1)}, u32[]{:S(2)}, u32[]{:S(2)}) %collective-permute-start.3) | collective-permute-done | bytes 196640 | tf_op jit(solution)/shard_map/ppermute | solution.py:41
  23.5 2.1 %collective-permute-start.8 = (bf16[128,768]{1,0:T(8,128)(2,1)S(1)}, bf16[128,768]{1,0:T(8,128)(2,1)S(1)}, u32[]{:S(2)}, u32[]{:S(2)}) collective-permute-start(bf16[128,768]{1,0:T(8,128)(2,1)S(1)} %collective-permute-done.5.refs_10_), channel_id=1, source_target_pairs={{0,4},{2,6},{4,8},{6,10},{8,12},{10,14},{12,0},{14,2},{1,5},{3,7},... | collective-permute-start | bytes 589832 | tf_op jit(solution)/shard_map/ppermute | solution.py:41
  25.6 0.7 %collective-permute-start.7 = (bf16[128,768]{1,0:T(8,128)(2,1)S(1)}, bf16[128,768]{1,0:T(8,128)(2,1)S(1)}, u32[]{:S(2)}, u32[]{:S(2)}) collective-permute-start(bf16[128,768]{1,0:T(8,128)(2,1)S(1)} %collective-permute-done.5.refs_10_), channel_id=1, source_target_pairs={{0,2},{2,0},{4,6},{6,4},{8,10},{10,8},{12,14},{14,12},{1,3},{3,1},... | collective-permute-start | bytes 589832 | tf_op jit(solution)/shard_map/ppermute | solution.py:41
  26.3 1.2 %collective-permute-start.6 = (bf16[128,768]{1,0:T(8,128)(2,1)S(1)}, bf16[128,768]{1,0:T(8,128)(2,1)S(1)}, u32[]{:S(2)}, u32[]{:S(2)}) collective-permute-start(bf16[128,768]{1,0:T(8,128)(2,1)S(1)} %collective-permute-done.5.refs_10_), channel_id=1, source_target_pairs={{0,16},{16,0},{1,17},{17,1},{2,18},{18,2},{3,19},{19,3},{4,20},{20... | collective-permute-start | bytes 589832 | tf_op jit(solution)/shard_map/ppermute | solution.py:41
  27.5 1.4 %collective-permute-done.29.refs_34_ = bf16[128,768]{1,0:T(8,128)(2,1)S(1)} collective-permute-done((bf16[128,768]{1,0:T(8,128)(2,1)S(1)}, bf16[128,768]{1,0:T(8,128)(2,1)S(1)}, u32[]{:S(2)}, u32[]{:S(2)}) %collective-permute-start.29) | collective-permute-done | bytes 196640 | tf_op jit(solution)/shard_map/ppermute | solution.py:41
  29.1 2.1 %collective-permute-start.11 = (bf16[128,768]{1,0:T(8,128)(2,1)S(1)}, bf16[128,768]{1,0:T(8,128)(2,1)}, u32[]{:S(2)}, u32[]{:S(2)}) collective-permute-start(bf16[128,768]{1,0:T(8,128)(2,1)S(1)} %collective-permute-done.4.refs_9_), channel_id=1, source_target_pairs={{0,4},{2,6},{4,8},{6,10},{8,12},{10,14},{12,0},{14,2},{1,5},{3,7},... | collective-permute-start | bytes 589832 | tf_op jit(solution)/shard_map/ppermute | solution.py:41
  32.0 1.3 %collective-permute-start.10 = (bf16[128,768]{1,0:T(8,128)(2,1)S(1)}, bf16[128,768]{1,0:T(8,128)(2,1)}, u32[]{:S(2)}, u32[]{:S(2)}) collective-permute-start(bf16[128,768]{1,0:T(8,128)(2,1)S(1)} %collective-permute-done.8.refs_13_), channel_id=1, source_target_pairs={{0,2},{2,0},{4,6},{6,4},{8,10},{10,8},{12,14},{14,12},{1,3},{3,1},... | collective-permute-start | bytes 589832 | tf_op jit(solution)/shard_map/ppermute | solution.py:41
  33.3 0.7 %and.23 = pred[256,16]{1,0:T(8,128)(4,1)} reshape(pred[16,1,256]{2,0,1:T(8,128)(4,1)S(1)} %and_and_fusion) | data formatting | bytes 8192 | tf_op jit(solution)/shard_map/and | solution.py:205
  34.0 0.9 %reduce_or.9 = pred[256]{0:T(512)(128)(4,1)S(1)} reduce(pred[256,16]{1,0:T(8,128)(4,1)} %and.23, pred[]{:T(512)} %constant.36.clone.1), dimensions={1}, to_apply=%region_1.0 | reduce | flops 3840 | bytes 4353 | tf_op jit(solution)/shard_map/reduce_or | solution.py:206
  34.9 1.5 %collective-permute-start.9 = (bf16[128,768]{1,0:T(8,128)(2,1)S(1)}, bf16[128,768]{1,0:T(8,128)(2,1)S(1)}, u32[]{:S(2)}, u32[]{:S(2)}) collective-permute-start(bf16[128,768]{1,0:T(8,128)(2,1)S(1)} %collective-permute-done.8.refs_13_), channel_id=1, source_target_pairs={{0,16},{16,0},{1,17},{17,1},{2,18},{18,2},{3,19},{19,3},{4,20},{20... | collective-permute-start | bytes 589832 | tf_op jit(solution)/shard_map/ppermute | solution.py:41
  36.9 3.2 %collective-permute-start.14 = (bf16[128,768]{1,0:T(8,128)(2,1)}, bf16[128,768]{1,0:T(8,128)(2,1)S(1)}, u32[]{:S(2)}, u32[]{:S(2)}) collective-permute-start(bf16[128,768]{1,0:T(8,128)(2,1)} %collective-permute-done.11.refs_16_), channel_id=1, source_target_pairs={{0,4},{2,6},{4,8},{6,10},{8,12},{10,14},{12,0},{14,2},{1,5},{3,7},... | collective-permute-start | bytes 589832 | tf_op jit(solution)/shard_map/ppermute | solution.py:41
  40.1 0.6 collective-permute-start.12
  40.6 0.9 %convert_multiply_fusion = f32[16,4,256]{2,1,0:T(4,128)S(1)} fusion(s32[16,4,256]{2,1,0:T(4,128)} %copy-done, f32[4]{0:T(128)} %constant.38.clone), kind=kLoop, calls=%fused_computation.2 | loop fusion | flops 32768 | bytes 131088 | tf_op jit(solution)/shard_map/mul | solution.py:208
  42.3 2.5 %collective-permute-done.14.refs_19_ = bf16[128,768]{1,0:T(8,128)(2,1)S(1)} collective-permute-done((bf16[128,768]{1,0:T(8,128)(2,1)}, bf16[128,768]{1,0:T(8,128)(2,1)S(1)}, u32[]{:S(2)}, u32[]{:S(2)}) %collective-permute-start.14) | collective-permute-done | bytes 196640 | tf_op jit(solution)/shard_map/ppermute | solution.py:41
  44.8 2.1 %collective-permute-done.12.refs_17_ = bf16[128,768]{1,0:T(8,128)(2,1)S(1)} collective-permute-done((bf16[128,768]{1,0:T(8,128)(2,1)}, bf16[128,768]{1,0:T(8,128)(2,1)S(1)}, u32[]{:S(2)}, u32[]{:S(2)}) %collective-permute-start.12) | collective-permute-done | bytes 196640 | tf_op jit(solution)/shard_map/ppermute | solution.py:41
  47.0 0.7 %dynamic-slice_bitcast_fusion.refs_1_ = s32[64]{0:T(128)S(1)} fusion(s32[32,64]{1,0:T(8,128)} %constant.39.clone, s32[]{:T(128)S(6)} %select_n.4), kind=kLoop, calls=%fused_computation.7 | loop fusion | bytes 516 | tf_op jit(solution)/shard_map/jit(dynamic_index_in_dim)/squeeze | solution.py:214
  47.7 0.6 collective-permute-done.28.refs_33_
  48.3 18.5 %spread.1 = f32[64,32,512]{2,1,0:T(8,128)} custom-call(s32[2]{0:T(128)S(1)} %pad_add_fusion.refs_0_, s32[64]{0:T(128)S(1)} %dynamic-slice_bitcast_fusion.refs_1_, s32[256]{0:T(256)S(1)} %convert_element_type.16.refs_2_, f32[16,8,256]{2,1,0:T(8,128)S(1)} %pad.4.refs_3_, bf16[128,768]{1,0:T(8,128)(2,1)S(1)} %bitcast.12, ...), custom_call_target="tpu_custom_call" | custom-call | tf_op jit(solution)/shard_map/spread/pallas_call | solution.py:174
  (50 shorter events, 3.1 us)
Async XLA Ops:
  1.0 6.7 %collective-permute-start.2 = (bf16[128,768]{1,0:T(8,128)(2,1)S(1)}, bf16[128,768]{1,0:T(8,128)(2,1)S(1)}, u32[]{:S(2)}, u32[]{:S(2)}) collective-permute-start(bf16[128,768]{1,0:T(8,128)(2,1)S(1)} %bitcast.8), channel_id=1, source_target_pairs={{0,4},{2,6},{4,8},{6,10},{8,12},{10,14},{12,0},{14,2},{1,5},{3,7},... | collective-permute-start | bytes 589832 | tf_op jit(solution)/shard_map/ppermute | solution.py:41
  2.6 13.6 %collective-permute-start.15 = (bf16[128,768]{1,0:T(8,128)(2,1)S(1)}, bf16[128,768]{1,0:T(8,128)(2,1)S(1)}, u32[]{:S(2)}, u32[]{:S(2)}) collective-permute-start(bf16[128,768]{1,0:T(8,128)(2,1)S(1)} %bitcast.9), channel_id=1, source_target_pairs={{0,1},{1,0},{2,3},{3,2},{4,5},{5,4},{6,7},{7,6},{8,9},{9,8},{10,11... | collective-permute-start | bytes 589832 | tf_op jit(solution)/shard_map/ppermute | solution.py:41
  2.6 15.2 %collective-permute-start.1 = (bf16[128,768]{1,0:T(8,128)(2,1)S(1)}, bf16[128,768]{1,0:T(8,128)(2,1)S(1)}, u32[]{:S(2)}, u32[]{:S(2)}) collective-permute-start(bf16[128,768]{1,0:T(8,128)(2,1)S(1)} %bitcast.10), channel_id=1, source_target_pairs={{0,2},{2,0},{4,6},{6,4},{8,10},{10,8},{12,14},{14,12},{1,3},{3,1},... | collective-permute-start | bytes 589832 | tf_op jit(solution)/shard_map/ppermute | solution.py:41
  4.1 14.8 %collective-permute-start = (bf16[128,768]{1,0:T(8,128)(2,1)S(1)}, bf16[128,768]{1,0:T(8,128)(2,1)S(1)}, u32[]{:S(2)}, u32[]{:S(2)}) collective-permute-start(bf16[128,768]{1,0:T(8,128)(2,1)S(1)} %bitcast.11), channel_id=1, source_target_pairs={{0,16},{16,0},{1,17},{17,1},{2,18},{18,2},{3,19},{19,3},{4,20},{20... | collective-permute-start | bytes 589832 | tf_op jit(solution)/shard_map/ppermute | solution.py:41
  7.7 11.3 %collective-permute-start.18 = (bf16[128,768]{1,0:T(8,128)(2,1)S(1)}, bf16[128,768]{1,0:T(8,128)(2,1)S(1)}, u32[]{:S(2)}, u32[]{:S(2)}) collective-permute-start(bf16[128,768]{1,0:T(8,128)(2,1)S(1)} %collective-permute-done.2.refs_7_), channel_id=1, source_target_pairs={{0,1},{1,0},{2,3},{3,2},{4,5},{5,4},{6,7},{7,6},{8,9},{9,8},{10,11... | collective-permute-start | bytes 589832 | tf_op jit(solution)/shard_map/ppermute | solution.py:41
  7.7 11.9 %collective-permute-start.13 = (bf16[128,768]{1,0:T(8,128)(2,1)S(1)}, bf16[128,768]{1,0:T(8,128)(2,1)S(1)}, u32[]{:S(2)}, u32[]{:S(2)}) collective-permute-start(bf16[128,768]{1,0:T(8,128)(2,1)S(1)} %collective-permute-done.2.refs_7_), channel_id=1, source_target_pairs={{0,2},{2,0},{4,6},{6,4},{8,10},{10,8},{12,14},{14,12},{1,3},{3,1},... | collective-permute-start | bytes 589832 | tf_op jit(solution)/shard_map/ppermute | solution.py:41
  16.2 5.9 %collective-permute-start.5 = (bf16[128,768]{1,0:T(8,128)(2,1)S(1)}, bf16[128,768]{1,0:T(8,128)(2,1)S(1)}, u32[]{:S(2)}, u32[]{:S(2)}) collective-permute-start(bf16[128,768]{1,0:T(8,128)(2,1)S(1)} %collective-permute-done.2.refs_7_), channel_id=1, source_target_pairs={{0,4},{2,6},{4,8},{6,10},{8,12},{10,14},{12,0},{14,2},{1,5},{3,7},... | collective-permute-start | bytes 589832 | tf_op jit(solution)/shard_map/ppermute | solution.py:41
  17.8 5.7 %collective-permute-start.3 = (bf16[128,768]{1,0:T(8,128)(2,1)S(1)}, bf16[128,768]{1,0:T(8,128)(2,1)S(1)}, u32[]{:S(2)}, u32[]{:S(2)}) collective-permute-start(bf16[128,768]{1,0:T(8,128)(2,1)S(1)} %collective-permute-done.2.refs_7_), channel_id=1, source_target_pairs={{0,16},{16,0},{1,17},{17,1},{2,18},{18,2},{3,19},{19,3},{4,20},{20... | collective-permute-start | bytes 589832 | tf_op jit(solution)/shard_map/ppermute | solution.py:41
  19.0 7.4 %collective-permute-start.16 = (bf16[128,768]{1,0:T(8,128)(2,1)S(1)}, bf16[128,768]{1,0:T(8,128)(2,1)S(1)}, u32[]{:S(2)}, u32[]{:S(2)}) collective-permute-start(bf16[128,768]{1,0:T(8,128)(2,1)S(1)} %collective-permute-done.refs_5_), channel_id=1, source_target_pairs={{0,1},{1,0},{2,3},{3,2},{4,5},{5,4},{6,7},{7,6},{8,9},{9,8},{10,11... | collective-permute-start | bytes 589832 | tf_op jit(solution)/shard_map/ppermute | solution.py:41
  19.0 8.5 %collective-permute-start.4 = (bf16[128,768]{1,0:T(8,128)(2,1)S(1)}, bf16[128,768]{1,0:T(8,128)(2,1)S(1)}, u32[]{:S(2)}, u32[]{:S(2)}) collective-permute-start(bf16[128,768]{1,0:T(8,128)(2,1)S(1)} %collective-permute-done.refs_5_), channel_id=1, source_target_pairs={{0,2},{2,0},{4,6},{6,4},{8,10},{10,8},{12,14},{14,12},{1,3},{3,1},... | collective-permute-start | bytes 589832 | tf_op jit(solution)/shard_map/ppermute | solution.py:41
  19.5 6.0 %collective-permute-start.17 = (bf16[128,768]{1,0:T(8,128)(2,1)S(1)}, bf16[128,768]{1,0:T(8,128)(2,1)S(1)}, u32[]{:S(2)}, u32[]{:S(2)}) collective-permute-start(bf16[128,768]{1,0:T(8,128)(2,1)S(1)} %collective-permute-done.1.refs_6_), channel_id=1, source_target_pairs={{0,1},{1,0},{2,3},{3,2},{4,5},{5,4},{6,7},{7,6},{8,9},{9,8},{10,11... | collective-permute-start | bytes 589832 | tf_op jit(solution)/shard_map/ppermute | solution.py:41
  21.5 10.5 %copy-start = (s32[16,4,256]{2,1,0:T(4,128)}, s32[16,4,256]{2,1,0:T(4,128)S(1)}, u32[]{:S(2)}) copy-start(s32[16,4,256]{2,1,0:T(4,128)S(1)} %multiply_reduce_fusion) | copy-start | bytes 196612
  22.1 6.9 %collective-permute-start.21 = (bf16[128,768]{1,0:T(8,128)(2,1)S(1)}, bf16[128,768]{1,0:T(8,128)(2,1)S(1)}, u32[]{:S(2)}, u32[]{:S(2)}) collective-permute-start(bf16[128,768]{1,0:T(8,128)(2,1)S(1)} %collective-permute-done.5.refs_10_), channel_id=1, source_target_pairs={{0,1},{1,0},{2,3},{3,2},{4,5},{5,4},{6,7},{7,6},{8,9},{9,8},{10,11... | collective-permute-start | bytes 589832 | tf_op jit(solution)/shard_map/ppermute | solution.py:41
  23.5 7.7 %collective-permute-start.8 = (bf16[128,768]{1,0:T(8,128)(2,1)S(1)}, bf16[128,768]{1,0:T(8,128)(2,1)S(1)}, u32[]{:S(2)}, u32[]{:S(2)}) collective-permute-start(bf16[128,768]{1,0:T(8,128)(2,1)S(1)} %collective-permute-done.5.refs_10_), channel_id=1, source_target_pairs={{0,4},{2,6},{4,8},{6,10},{8,12},{10,14},{12,0},{14,2},{1,5},{3,7},... | collective-permute-start | bytes 589832 | tf_op jit(solution)/shard_map/ppermute | solution.py:41
  25.6 5.7 %collective-permute-start.7 = (bf16[128,768]{1,0:T(8,128)(2,1)S(1)}, bf16[128,768]{1,0:T(8,128)(2,1)S(1)}, u32[]{:S(2)}, u32[]{:S(2)}) collective-permute-start(bf16[128,768]{1,0:T(8,128)(2,1)S(1)} %collective-permute-done.5.refs_10_), channel_id=1, source_target_pairs={{0,2},{2,0},{4,6},{6,4},{8,10},{10,8},{12,14},{14,12},{1,3},{3,1},... | collective-permute-start | bytes 589832 | tf_op jit(solution)/shard_map/ppermute | solution.py:41
  26.3 5.7 %collective-permute-start.6 = (bf16[128,768]{1,0:T(8,128)(2,1)S(1)}, bf16[128,768]{1,0:T(8,128)(2,1)S(1)}, u32[]{:S(2)}, u32[]{:S(2)}) collective-permute-start(bf16[128,768]{1,0:T(8,128)(2,1)S(1)} %collective-permute-done.5.refs_10_), channel_id=1, source_target_pairs={{0,16},{16,0},{1,17},{17,1},{2,18},{18,2},{3,19},{19,3},{4,20},{20... | collective-permute-start | bytes 589832 | tf_op jit(solution)/shard_map/ppermute | solution.py:41
  27.5 1.4 %collective-permute-start.29 = (bf16[128,768]{1,0:T(8,128)(2,1)S(1)}, bf16[128,768]{1,0:T(8,128)(2,1)S(1)}, u32[]{:S(2)}, u32[]{:S(2)}) collective-permute-start(bf16[128,768]{1,0:T(8,128)(2,1)S(1)} %collective-permute-done.13.refs_18_), channel_id=1, source_target_pairs={{0,1},{1,0},{2,3},{3,2},{4,5},{5,4},{6,7},{7,6},{8,9},{9,8},{10,11... | collective-permute-start | bytes 589832 | tf_op jit(solution)/shard_map/ppermute | solution.py:41
  28.9 7.4 %collective-permute-start.20 = (bf16[128,768]{1,0:T(8,128)(2,1)S(1)}, bf16[128,768]{1,0:T(8,128)(2,1)S(1)}, u32[]{:S(2)}, u32[]{:S(2)}) collective-permute-start(bf16[128,768]{1,0:T(8,128)(2,1)S(1)} %collective-permute-done.4.refs_9_), channel_id=1, source_target_pairs={{0,1},{1,0},{2,3},{3,2},{4,5},{5,4},{6,7},{7,6},{8,9},{9,8},{10,11... | collective-permute-start | bytes 589832 | tf_op jit(solution)/shard_map/ppermute | solution.py:41
  29.1 7.3 %collective-permute-start.11 = (bf16[128,768]{1,0:T(8,128)(2,1)S(1)}, bf16[128,768]{1,0:T(8,128)(2,1)}, u32[]{:S(2)}, u32[]{:S(2)}) collective-permute-start(bf16[128,768]{1,0:T(8,128)(2,1)S(1)} %collective-permute-done.4.refs_9_), channel_id=1, source_target_pairs={{0,4},{2,6},{4,8},{6,10},{8,12},{10,14},{12,0},{14,2},{1,5},{3,7},... | collective-permute-start | bytes 589832 | tf_op jit(solution)/shard_map/ppermute | solution.py:41
  31.2 3.8 %collective-permute-start.19 = (bf16[128,768]{1,0:T(8,128)(2,1)S(1)}, bf16[128,768]{1,0:T(8,128)(2,1)}, u32[]{:S(2)}, u32[]{:S(2)}) collective-permute-start(bf16[128,768]{1,0:T(8,128)(2,1)S(1)} %collective-permute-done.3.refs_8_), channel_id=1, source_target_pairs={{0,1},{1,0},{2,3},{3,2},{4,5},{5,4},{6,7},{7,6},{8,9},{9,8},{10,11... | collective-permute-start | bytes 589832 | tf_op jit(solution)/shard_map/ppermute | solution.py:41
  31.3 5.6 %collective-permute-start.24 = (bf16[128,768]{1,0:T(8,128)(2,1)S(1)}, bf16[128,768]{1,0:T(8,128)(2,1)}, u32[]{:S(2)}, u32[]{:S(2)}) collective-permute-start(bf16[128,768]{1,0:T(8,128)(2,1)S(1)} %collective-permute-done.8.refs_13_), channel_id=1, source_target_pairs={{0,1},{1,0},{2,3},{3,2},{4,5},{5,4},{6,7},{7,6},{8,9},{9,8},{10,11... | collective-permute-start | bytes 589832 | tf_op jit(solution)/shard_map/ppermute | solution.py:41
  32.0 8.1 %collective-permute-start.10 = (bf16[128,768]{1,0:T(8,128)(2,1)S(1)}, bf16[128,768]{1,0:T(8,128)(2,1)}, u32[]{:S(2)}, u32[]{:S(2)}) collective-permute-start(bf16[128,768]{1,0:T(8,128)(2,1)S(1)} %collective-permute-done.8.refs_13_), channel_id=1, source_target_pairs={{0,2},{2,0},{4,6},{6,4},{8,10},{10,8},{12,14},{14,12},{1,3},{3,1},... | collective-permute-start | bytes 589832 | tf_op jit(solution)/shard_map/ppermute | solution.py:41
  34.9 6.7 %collective-permute-start.9 = (bf16[128,768]{1,0:T(8,128)(2,1)S(1)}, bf16[128,768]{1,0:T(8,128)(2,1)S(1)}, u32[]{:S(2)}, u32[]{:S(2)}) collective-permute-start(bf16[128,768]{1,0:T(8,128)(2,1)S(1)} %collective-permute-done.8.refs_13_), channel_id=1, source_target_pairs={{0,16},{16,0},{1,17},{17,1},{2,18},{18,2},{3,19},{19,3},{4,20},{20... | collective-permute-start | bytes 589832 | tf_op jit(solution)/shard_map/ppermute | solution.py:41
  36.4 5.3 %collective-permute-start.23 = (bf16[128,768]{1,0:T(8,128)(2,1)S(1)}, bf16[128,768]{1,0:T(8,128)(2,1)S(1)}, u32[]{:S(2)}, u32[]{:S(2)}) collective-permute-start(bf16[128,768]{1,0:T(8,128)(2,1)S(1)} %collective-permute-done.7.refs_12_), channel_id=1, source_target_pairs={{0,1},{1,0},{2,3},{3,2},{4,5},{5,4},{6,7},{7,6},{8,9},{9,8},{10,11... | collective-permute-start | bytes 589832 | tf_op jit(solution)/shard_map/ppermute | solution.py:41
  36.4 5.8 %collective-permute-start.22 = (bf16[128,768]{1,0:T(8,128)(2,1)S(1)}, bf16[128,768]{1,0:T(8,128)(2,1)S(1)}, u32[]{:S(2)}, u32[]{:S(2)}) collective-permute-start(bf16[128,768]{1,0:T(8,128)(2,1)S(1)} %collective-permute-done.6.refs_11_), channel_id=1, source_target_pairs={{0,1},{1,0},{2,3},{3,2},{4,5},{5,4},{6,7},{7,6},{8,9},{9,8},{10,11... | collective-permute-start | bytes 589832 | tf_op jit(solution)/shard_map/ppermute | solution.py:41
  36.9 7.9 %collective-permute-start.14 = (bf16[128,768]{1,0:T(8,128)(2,1)}, bf16[128,768]{1,0:T(8,128)(2,1)S(1)}, u32[]{:S(2)}, u32[]{:S(2)}) collective-permute-start(bf16[128,768]{1,0:T(8,128)(2,1)} %collective-permute-done.11.refs_16_), channel_id=1, source_target_pairs={{0,4},{2,6},{4,8},{6,10},{8,12},{10,14},{12,0},{14,2},{1,5},{3,7},... | collective-permute-start | bytes 589832 | tf_op jit(solution)/shard_map/ppermute | solution.py:41
  40.1 6.8 %collective-permute-start.12 = (bf16[128,768]{1,0:T(8,128)(2,1)}, bf16[128,768]{1,0:T(8,128)(2,1)S(1)}, u32[]{:S(2)}, u32[]{:S(2)}) collective-permute-start(bf16[128,768]{1,0:T(8,128)(2,1)} %collective-permute-done.10.refs_15_), channel_id=1, source_target_pairs={{0,16},{16,0},{1,17},{17,1},{2,18},{18,2},{3,19},{19,3},{4,20},{20... | collective-permute-start | bytes 589832 | tf_op jit(solution)/shard_map/ppermute | solution.py:41
  41.6 6.1 %collective-permute-start.27 = (bf16[128,768]{1,0:T(8,128)(2,1)}, bf16[128,768]{1,0:T(8,128)(2,1)S(1)}, u32[]{:S(2)}, u32[]{:S(2)}) collective-permute-start(bf16[128,768]{1,0:T(8,128)(2,1)} %collective-permute-done.11.refs_16_), channel_id=1, source_target_pairs={{0,1},{1,0},{2,3},{3,2},{4,5},{5,4},{6,7},{7,6},{8,9},{9,8},{10,11... | collective-permute-start | bytes 589832 | tf_op jit(solution)/shard_map/ppermute | solution.py:41
  41.7 6.0 %collective-permute-start.26 = (bf16[128,768]{1,0:T(8,128)(2,1)}, bf16[128,768]{1,0:T(8,128)(2,1)S(1)}, u32[]{:S(2)}, u32[]{:S(2)}) collective-permute-start(bf16[128,768]{1,0:T(8,128)(2,1)} %collective-permute-done.10.refs_15_), channel_id=1, source_target_pairs={{0,1},{1,0},{2,3},{3,2},{4,5},{5,4},{6,7},{7,6},{8,9},{9,8},{10,11... | collective-permute-start | bytes 589832 | tf_op jit(solution)/shard_map/ppermute | solution.py:41
  42.2 5.5 %collective-permute-start.25 = (bf16[128,768]{1,0:T(8,128)(2,1)S(1)}, bf16[128,768]{1,0:T(8,128)(2,1)S(1)}, u32[]{:S(2)}, u32[]{:S(2)}) collective-permute-start(bf16[128,768]{1,0:T(8,128)(2,1)S(1)} %collective-permute-done.9.refs_14_), channel_id=1, source_target_pairs={{0,1},{1,0},{2,3},{3,2},{4,5},{5,4},{6,7},{7,6},{8,9},{9,8},{10,11... | collective-permute-start | bytes 589832 | tf_op jit(solution)/shard_map/ppermute | solution.py:41
  44.8 2.9 %collective-permute-start.30 = (bf16[128,768]{1,0:T(8,128)(2,1)S(1)}, bf16[128,768]{1,0:T(8,128)(2,1)S(1)}, u32[]{:S(2)}, u32[]{:S(2)}) collective-permute-start(bf16[128,768]{1,0:T(8,128)(2,1)S(1)} %collective-permute-done.14.refs_19_), channel_id=1, source_target_pairs={{0,1},{1,0},{2,3},{3,2},{4,5},{5,4},{6,7},{7,6},{8,9},{9,8},{10,11... | collective-permute-start | bytes 589832 | tf_op jit(solution)/shard_map/ppermute | solution.py:41
  46.9 1.4 %collective-permute-start.28 = (bf16[128,768]{1,0:T(8,128)(2,1)S(1)}, bf16[128,768]{1,0:T(8,128)(2,1)S(1)}, u32[]{:S(2)}, u32[]{:S(2)}) collective-permute-start(bf16[128,768]{1,0:T(8,128)(2,1)S(1)} %collective-permute-done.12.refs_17_), channel_id=1, source_target_pairs={{0,1},{1,0},{2,3},{3,2},{4,5},{5,4},{6,7},{7,6},{8,9},{9,8},{10,11... | collective-permute-start | bytes 589832 | tf_op jit(solution)/shard_map/ppermute | solution.py:41
